TPU v7x, 32 devices: a whole 2x2x4 slice. The times are simulated.
32 devices in a mesh: row: 8 (over z, y), kk: 4 (over x, core).
Axes of the slice: x: 2, y: 2, z: 4, core: 2. Of those that a mesh axis runs over, the one named last changes fastest.
Arguments:
- left_blocks: bfloat16 [4096, 4096], P('row', 'kk'), may hold values from -6 to 6
- right_blocks: bfloat16 [4096, 1024], P('kk', 'row'), may hold values from -0.125 to 0.125
- left_mask: int32 [32, 32], P('row', 'kk'), may hold values 0 or 1
- right_mask: int32 [32, 8], P('kk', 'row'), may hold values 0 or 1
- out_mask: int32 [32, 8], P('row'), may hold values 0 or 1
Outputs:
- product_blocks: bfloat16 [4096, 1024], P(('row', 'kk'))
All inputs are finite; a program needn't handle non-finite values. No bound on the sum of `left_mask` or of `right_mask` or of `out_mask` on one device may be relied on, other than what follows from the above.
Results may differ from a plain program's by a relative error of at most 0.001.
Values may be sent and summed in bfloat16 or wider, within the bound.
A program may use at most 192 MiB of HBM per device.

v0:
```python
import jax
import jax.numpy as jnp
from jax import lax
from jax.sharding import PartitionSpec as P


def expand(mask, size):
    return jnp.repeat(jnp.repeat(mask, size, axis=0), size, axis=1)


def per_device(left_blocks, right_blocks, left_mask, right_mask, out_mask):
    block = left_blocks.shape[0] // left_mask.shape[0]
    left_used = left_blocks * expand(left_mask, block).astype(jnp.bfloat16)
    right_used = right_blocks * expand(right_mask, block).astype(jnp.bfloat16)
    share = left_used.shape[0] // lax.axis_size("kk")
    right_all = lax.all_gather(right_used, "row", axis=1, tiled=True)
    summed = lax.psum_scatter(
        jnp.dot(left_used, right_all, preferred_element_type=jnp.float32),
        "kk",
        scatter_dimension=0,
        tiled=True,
    )
    mask_rows = expand(out_mask, block).astype(jnp.float32)
    own_mask = lax.dynamic_slice_in_dim(mask_rows, lax.axis_index("kk") * share, share, 0)
    return (summed * own_mask).astype(jnp.bfloat16)


def solution(mesh):
    in_specs = (P("row", "kk"), P("kk", "row"), P("row", "kk"), P("kk", "row"), P("row", None))
    out_specs = P(("row", "kk"), None)
    return jax.shard_map(
        per_device, mesh=mesh, in_specs=in_specs, out_specs=out_specs, check_vma=False
    )
```

profile of v0, /device:TPU:0, one launch (start us, length us, event | category | flops | bytes accessed | tf_op | source)
XLA Modules:
  0.0 105.5 jit_solution(10613878520376923319)
XLA Ops:
  6.5 0.0 copy-start.1
  6.5 0.0 all-gather.2.cloned.1.call-start
  6.5 0.7 convert_bitcast_fusion
  7.3 0.1 broadcast_bitcast_fusion
  7.4 1.9 %broadcast_multiply_fusion = bf16[1024,128]{1,0:T(8,128)(2,1)} fusion(bf16[1024,128]{1,0:T(8,128)(2,1)} %param.6, bf16[1024]{0:T(1024)(128)(2,1)S(1)} %broadcast_bitcast_fusion), kind=kLoop, calls=%fused_computation.5 | loop fusion | flops 131072 | bytes 526336 | tf_op jit(solution)/shard_map/mul | solution.py:14
  9.2 0.0 all-gather.2.cloned.1.call-update
  9.2 0.0 reduce-scatter.2.cloned.1.call-start
  9.3 0.7 convert_element_type.36
  10.0 52.5 %all-gather.2.cloned.1.call-done = bf16[1024,1024]{1,0:T(8,128)(2,1)} async-done(((bf16[1024,128]{1,0:T(8,128)(2,1)}), bf16[1024,1024]{1,0:T(8,128)(2,1)}) %all-gather.2.cloned.1.call-update) | async-done | bytes 2097168 | tf_op jit(solution)/shard_map/all_gather | solution.py:16
  62.5 0.6 broadcast_in_dim.17
  63.1 0.0 copy-done.1
  63.1 4.2 %fusion = f32[512,1024]{1,0:T(8,128)} fusion(bf16[1024,1024]{1,0:T(8,128)(2,1)} %all-gather.2.cloned.1.call-done, bf16[512,1024]{1,0:T(8,128)(2,1)S(1)} %copy-done.1, bf16[64,8,8,128]{3,2,1,0:T(8,128)(2,1)S(1)} %bitcast.18), kind=kOutput, calls=%fused_computation.2 | convolution fusion | flops 1074266112 | bytes 6291456 | tf_op jit(solution)/shard_map/dot_general | solution.py:18
  67.3 0.0 copy-start
  67.3 0.0 reduce-scatter.2.cloned.1.call-update
  67.4 0.7 copy-done
  68.0 0.6 broadcast_in_dim.20
  68.6 0.5 copy.13
  69.1 27.7 %reduce-scatter.2.cloned.1.call-done = f32[128,1024]{1,0:T(8,128)} async-done(((f32[512,1024]{1,0:T(8,128)}), f32[128,1024]{1,0:T(8,128)}) %reduce-scatter.2.cloned.1.call-update) | async-done | bytes 524304 | tf_op jit(solution)/shard_map/reduce_scatter | solution.py:17
  96.8 1.8 %multiply_convert_fusion = bf16[128,1024]{1,0:T(8,128)(2,1)} fusion(f32[128,1024]{1,0:T(8,128)} %reduce-scatter.2.cloned.1.call-done, f32[512,1024]{1,0:T(8,128)S(1)} %bitcast.16, s32[]{:T(128)S(6)} %select_n.3), kind=kLoop, calls=%fused_computation.4 | loop fusion | flops 262144 | bytes 1310724 | tf_op jit(solution)/shard_map/convert_element_type | solution.py:25
  (3 shorter events, 0.0 us)
Async XLA Ops:
  6.5 56.6 %copy-start.1 = (bf16[512,1024]{1,0:T(8,128)(2,1)S(1)}, bf16[512,1024]{1,0:T(8,128)(2,1)}, u32[]{:S(2)}) copy-start(bf16[512,1024]{1,0:T(8,128)(2,1)} %param.5) | copy-start | bytes 3145732
  6.5 55.9 %all-gather.2.cloned.1.call-start = ((), (), s32[]{:S(2)}) async-start(), calls=%async_computation.1 | async-start | bytes 2359296 | tf_op jit(solution)/shard_map/all_gather | solution.py:16
  9.2 87.6 %reduce-scatter.2.cloned.1.call-start = ((), (), s32[]{:S(2)}) async-start(), calls=%async_computation.2 | async-start | bytes 2621440 | tf_op jit(solution)/shard_map/reduce_scatter | solution.py:17
  67.3 0.7 copy-start
Sparse Core Ops, SparseCore 0:
  9.4 53.0 all-gather.1
  67.5 29.3 reduce-scatter.1
where the time goes:
time: 106 us; the launch traced here: 105 us
  waiting for transfers between devices  80.3 us (76%)
  between operations  13.4 us (13%)
  other arithmetic  5.09 us (5%)
  matrix products  4.2 us (4%)
  local copies, waits for them, and re-layouts  2.44 us (2%)
    all_gather x1, waiting for transfers between devices, per_device(): right_all = lax.all_gather(right_used, 'row', axis=1, tiled=True)  52.5 us
    reduce_scatter x1, waiting for transfers between devices, per_device(): lax.psum_scatter(jnp.dot(left_used, right_all, preferred_element_type=jnp...  27.7 us
    dot_general x1, matrix products, per_device(): jnp.dot(left_used, right_all, preferred_element_type=jnp.float32)  4.2 us
  transfers between devices with their start and end apart: 2, of which 2 were waited for; matrix products, arithmetic and copies ran while one was open for 2% of the time, Pallas kernels for 0%

commit v1 on v0

--- a/solution.py
+++ b/solution.py
@@ -13,7 +13,12 @@
     left_used = left_blocks * expand(left_mask, block).astype(jnp.bfloat16)
     right_used = right_blocks * expand(right_mask, block).astype(jnp.bfloat16)
     share = left_used.shape[0] // lax.axis_size("kk")
-    right_all = lax.all_gather(right_used, "row", axis=1, tiled=True)
+    ring = [right_used]
+    for hop in range(7):
+        ring.append(lax.ppermute(ring[-1], "row", [(dev, (dev + 1) % 8) for dev in range(8)]))
+    right_all = jnp.roll(
+        jnp.concatenate(ring[::-1], axis=1), (lax.axis_index("row") + 1) * ring[0].shape[1], axis=1
+    )
     summed = lax.psum_scatter(
         jnp.dot(left_used, right_all, preferred_element_type=jnp.float32),
         "kk",

time: 106 us -> 120 us (1.13)
  waiting for transfers between devices: 80.3 us -> 92.3 us
  starting transfers between devices: 0.04 us -> 3.07 us
  matrix products: 4.2 us -> 2.62 us
    ppermute x0 -> x7, waiting for transfers between devices: none -> 65 us  [per_device(): lax.ppermute(ring[-1], 'row', [(dev, (dev + 1) % 8) for dev in range(8)])]
    all_gather x1 -> x0, waiting for transfers between devices: 52.5 us -> none  [per_device(): right_all = lax.all_gather(right_used, 'row', axis=1, tiled=True)]
    ppermute x0 -> x7, starting transfers between devices: none -> 3.06 us  [per_device(): lax.ppermute(ring[-1], 'row', [(dev, (dev + 1) % 8) for dev in range(8)])]
    dot_general x1, matrix products: 4.2 us -> 2.62 us  [per_device(): jnp.dot(left_used, right_all, preferred_element_type=jnp.float32)]
  transfers between devices with their start and end apart: 2 -> 8, of which waited for: 2 -> 8; matrix products, arithmetic and copies ran while one was open for 2% -> 1% of each run, Pallas kernels for 0% -> 0%
where the time goes in v1:
time: 120 us; the launch traced here: 119 us
  waiting for transfers between devices  92.3 us (77%)
  between operations  13.6 us (11%)
  other arithmetic  4.87 us (4%)
  starting transfers between devices  3.07 us (3%)
  local copies, waits for them, and re-layouts  2.98 us (2%)
  matrix products  2.62 us (2%)
    ppermute x7, waiting for transfers between devices, per_device(): lax.ppermute(ring[-1], 'row', [(dev, (dev + 1) % 8) for dev in range(8)])  65 us
    reduce_scatter x1, waiting for transfers between devices, per_device(): lax.psum_scatter(jnp.dot(left_used, right_all, preferred_element_type=jnp...  27.3 us
    ppermute x7, starting transfers between devices, per_device(): lax.ppermute(ring[-1], 'row', [(dev, (dev + 1) % 8) for dev in range(8)])  3.06 us
    dot_general x1, matrix products, per_device(): jnp.dot(left_used, right_all, preferred_element_type=jnp.float32)  2.62 us
  transfers between devices with their start and end apart: 8, of which 8 were waited for; matrix products, arithmetic and copies ran while one was open for 1% of the time, Pallas kernels for 0%

profile of v1, /device:TPU:0, one launch (start us, length us, event | category | flops | bytes accessed | tf_op | source)
XLA Modules:
  0.0 119.5 jit_solution(14429798386551561590)
XLA Ops:
  6.5 0.7 convert_bitcast_fusion
  7.3 1.1 broadcast_multiply_fusion
  8.5 3.0 %collective-permute-start = (bf16[1024,128]{1,0:T(8,128)(2,1)S(1)}, bf16[1024,128]{1,0:T(8,128)(2,1)S(1)}, u32[]{:S(2)}, u32[]{:S(2)}) collective-permute-start(bf16[1024,128]{1,0:T(8,128)(2,1)S(1)} %broadcast_multiply_fusion), channel_id=1, source_target_pairs={{0,4},{4,8},{8,12},{12,16},{16,20},{20,24},{24,28},{28,0},{1,5},{5... | collective-permute-start | bytes 786440 | tf_op jit(solution)/shard_map/ppermute | solution.py:18
  11.5 9.3 %collective-permute-done = bf16[1024,128]{1,0:T(8,128)(2,1)S(1)} collective-permute-done((bf16[1024,128]{1,0:T(8,128)(2,1)S(1)}, bf16[1024,128]{1,0:T(8,128)(2,1)S(1)}, u32[]{:S(2)}, u32[]{:S(2)}) %collective-permute-start) | collective-permute-done | bytes 262176 | tf_op jit(solution)/shard_map/ppermute | solution.py:18
  20.9 10.2 %collective-permute-done.1 = bf16[1024,128]{1,0:T(8,128)(2,1)S(1)} collective-permute-done((bf16[1024,128]{1,0:T(8,128)(2,1)S(1)}, bf16[1024,128]{1,0:T(8,128)(2,1)S(1)}, u32[]{:S(2)}, u32[]{:S(2)}) %collective-permute-start.1) | collective-permute-done | bytes 262176 | tf_op jit(solution)/shard_map/ppermute | solution.py:18
  31.0 9.3 %collective-permute-done.2 = bf16[1024,128]{1,0:T(8,128)(2,1)S(1)} collective-permute-done((bf16[1024,128]{1,0:T(8,128)(2,1)S(1)}, bf16[1024,128]{1,0:T(8,128)(2,1)S(1)}, u32[]{:S(2)}, u32[]{:S(2)}) %collective-permute-start.2) | collective-permute-done | bytes 262176 | tf_op jit(solution)/shard_map/ppermute | solution.py:18
  40.3 9.1 %collective-permute-done.3 = bf16[1024,128]{1,0:T(8,128)(2,1)S(1)} collective-permute-done((bf16[1024,128]{1,0:T(8,128)(2,1)S(1)}, bf16[1024,128]{1,0:T(8,128)(2,1)S(1)}, u32[]{:S(2)}, u32[]{:S(2)}) %collective-permute-start.3) | collective-permute-done | bytes 262176 | tf_op jit(solution)/shard_map/ppermute | solution.py:18
  49.4 9.1 %collective-permute-done.4 = bf16[1024,128]{1,0:T(8,128)(2,1)S(1)} collective-permute-done((bf16[1024,128]{1,0:T(8,128)(2,1)S(1)}, bf16[1024,128]{1,0:T(8,128)(2,1)S(1)}, u32[]{:S(2)}, u32[]{:S(2)}) %collective-permute-start.4) | collective-permute-done | bytes 262176 | tf_op jit(solution)/shard_map/ppermute | solution.py:18
  58.5 9.7 %collective-permute-done.5 = bf16[1024,128]{1,0:T(8,128)(2,1)S(1)} collective-permute-done((bf16[1024,128]{1,0:T(8,128)(2,1)S(1)}, bf16[1024,128]{1,0:T(8,128)(2,1)S(1)}, u32[]{:S(2)}, u32[]{:S(2)}) %collective-permute-start.5) | collective-permute-done | bytes 262176 | tf_op jit(solution)/shard_map/ppermute | solution.py:18
  68.2 0.7 convert_element_type.36
  68.8 8.4 %collective-permute-done.6 = bf16[1024,128]{1,0:T(8,128)(2,1)S(1)} collective-permute-done((bf16[1024,128]{1,0:T(8,128)(2,1)S(1)}, bf16[1024,128]{1,0:T(8,128)(2,1)S(1)}, u32[]{:S(2)}, u32[]{:S(2)}) %collective-permute-start.6) | collective-permute-done | bytes 262176 | tf_op jit(solution)/shard_map/ppermute | solution.py:18
  77.3 0.1 constant_dynamic-update-slice_fusion.14
  77.4 0.1 constant_dynamic-update-slice_fusion.13
  77.6 0.1 constant_dynamic-update-slice_fusion.11
  77.8 0.1 constant_dynamic-update-slice_fusion.9
  77.9 0.3 constant_dynamic-update-slice_fusion.8
  78.2 0.1 constant_dynamic-update-slice_fusion.6
  78.8 0.3 constant_dynamic-update-slice_fusion
  79.1 0.6 broadcast_in_dim.17
  79.7 2.6 %fusion = f32[512,1024]{1,0:T(8,128)} fusion(bf16[1024,2048]{1,0:T(8,128)(2,1)S(1)} %constant_dynamic-update-slice_fusion, s32[]{:T(128)S(6)} %select_n.17, bf16[512,1024]{1,0:T(8,128)(2,1)S(1)} %copy-done.2, bf16[64,8,8,128]{3,2,1,0:T(8,128)(2,1)S(1)} %bitcast.17), kind=kOutput, calls=%fused_computation.1 | convolution fusion | flops 1074266112 | bytes 6291460 | tf_op jit(solution)/shard_map/dot_general | solution.py:23
  82.4 0.6 broadcast_in_dim.20
  83.0 0.5 copy.13
  83.5 27.3 %reduce-scatter.2.cloned.1.call-done = f32[128,1024]{1,0:T(8,128)} async-done(((f32[512,1024]{1,0:T(8,128)}), f32[128,1024]{1,0:T(8,128)}) %reduce-scatter.2.cloned.1.call-update) | async-done | bytes 524304 | tf_op jit(solution)/shard_map/reduce_scatter | solution.py:22
  110.8 1.8 %multiply_convert_fusion = bf16[128,1024]{1,0:T(8,128)(2,1)} fusion(f32[128,1024]{1,0:T(8,128)} %reduce-scatter.2.cloned.1.call-done, f32[512,1024]{1,0:T(8,128)S(1)} %bitcast.15, s32[]{:T(128)S(6)} %select_n.18), kind=kLoop, calls=%fused_computation.5 | loop fusion | flops 262144 | bytes 1310724 | tf_op jit(solution)/shard_map/convert_element_type | solution.py:30
  (27 shorter events, 0.9 us)
Async XLA Ops:
  6.5 71.3 %copy-start = (bf16[1024,128]{1,0:T(8,128)(2,1)S(1)}, bf16[1024,128]{1,0:T(8,128)(2,1)}, u32[]{:S(2)}) copy-start(bf16[1024,128]{1,0:T(8,128)(2,1)} %param.6) | copy-start | bytes 786436
  6.5 104.3 %reduce-scatter.2.cloned.1.call-start = ((), (), s32[]{:S(2)}) async-start(), calls=%async_computation.1 | async-start | bytes 2621440 | tf_op jit(solution)/shard_map/reduce_scatter | solution.py:22
  8.5 12.4 %collective-permute-start = (bf16[1024,128]{1,0:T(8,128)(2,1)S(1)}, bf16[1024,128]{1,0:T(8,128)(2,1)S(1)}, u32[]{:S(2)}, u32[]{:S(2)}) collective-permute-start(bf16[1024,128]{1,0:T(8,128)(2,1)S(1)} %broadcast_multiply_fusion), channel_id=1, source_target_pairs={{0,4},{4,8},{8,12},{12,16},{16,20},{20,24},{24,28},{28,0},{1,5},{5... | collective-permute-start | bytes 786440 | tf_op jit(solution)/shard_map/ppermute | solution.py:18
  20.9 10.2 %collective-permute-start.1 = (bf16[1024,128]{1,0:T(8,128)(2,1)S(1)}, bf16[1024,128]{1,0:T(8,128)(2,1)S(1)}, u32[]{:S(2)}, u32[]{:S(2)}) collective-permute-start(bf16[1024,128]{1,0:T(8,128)(2,1)S(1)} %collective-permute-done), channel_id=1, source_target_pairs={{0,4},{4,8},{8,12},{12,16},{16,20},{20,24},{24,28},{28,0},{1,5},{5... | collective-permute-start | bytes 786440 | tf_op jit(solution)/shard_map/ppermute | solution.py:18
  31.0 9.3 %collective-permute-start.2 = (bf16[1024,128]{1,0:T(8,128)(2,1)S(1)}, bf16[1024,128]{1,0:T(8,128)(2,1)S(1)}, u32[]{:S(2)}, u32[]{:S(2)}) collective-permute-start(bf16[1024,128]{1,0:T(8,128)(2,1)S(1)} %collective-permute-done.1), channel_id=1, source_target_pairs={{0,4},{4,8},{8,12},{12,16},{16,20},{20,24},{24,28},{28,0},{1,5},{5... | collective-permute-start | bytes 786440 | tf_op jit(solution)/shard_map/ppermute | solution.py:18
  40.3 9.1 %collective-permute-start.3 = (bf16[1024,128]{1,0:T(8,128)(2,1)S(1)}, bf16[1024,128]{1,0:T(8,128)(2,1)S(1)}, u32[]{:S(2)}, u32[]{:S(2)}) collective-permute-start(bf16[1024,128]{1,0:T(8,128)(2,1)S(1)} %collective-permute-done.2), channel_id=1, source_target_pairs={{0,4},{4,8},{8,12},{12,16},{16,20},{20,24},{24,28},{28,0},{1,5},{5... | collective-permute-start | bytes 786440 | tf_op jit(solution)/shard_map/ppermute | solution.py:18
  49.4 9.1 %collective-permute-start.4 = (bf16[1024,128]{1,0:T(8,128)(2,1)S(1)}, bf16[1024,128]{1,0:T(8,128)(2,1)S(1)}, u32[]{:S(2)}, u32[]{:S(2)}) collective-permute-start(bf16[1024,128]{1,0:T(8,128)(2,1)S(1)} %collective-permute-done.3), channel_id=1, source_target_pairs={{0,4},{4,8},{8,12},{12,16},{16,20},{20,24},{24,28},{28,0},{1,5},{5... | collective-permute-start | bytes 786440 | tf_op jit(solution)/shard_map/ppermute | solution.py:18
  58.5 9.7 %collective-permute-start.5 = (bf16[1024,128]{1,0:T(8,128)(2,1)S(1)}, bf16[1024,128]{1,0:T(8,128)(2,1)S(1)}, u32[]{:S(2)}, u32[]{:S(2)}) collective-permute-start(bf16[1024,128]{1,0:T(8,128)(2,1)S(1)} %collective-permute-done.4), channel_id=1, source_target_pairs={{0,4},{4,8},{8,12},{12,16},{16,20},{20,24},{24,28},{28,0},{1,5},{5... | collective-permute-start | bytes 786440 | tf_op jit(solution)/shard_map/ppermute | solution.py:18
  68.2 9.1 %collective-permute-start.6 = (bf16[1024,128]{1,0:T(8,128)(2,1)S(1)}, bf16[1024,128]{1,0:T(8,128)(2,1)S(1)}, u32[]{:S(2)}, u32[]{:S(2)}) collective-permute-start(bf16[1024,128]{1,0:T(8,128)(2,1)S(1)} %collective-permute-done.5), channel_id=1, source_target_pairs={{0,4},{4,8},{8,12},{12,16},{16,20},{20,24},{24,28},{28,0},{1,5},{5... | collective-permute-start | bytes 786440 | tf_op jit(solution)/shard_map/ppermute | solution.py:18
  77.5 2.2 %copy-start.2 = (bf16[512,1024]{1,0:T(8,128)(2,1)S(1)}, bf16[512,1024]{1,0:T(8,128)(2,1)}, u32[]{:S(2)}) copy-start(bf16[512,1024]{1,0:T(8,128)(2,1)} %param.5) | copy-start | bytes 3145732
  79.7 2.7 %copy-start.1 = (s32[4,8]{1,0:T(4,128)S(1)}, s32[4,8]{1,0:T(4,128)}, u32[]{:S(2)}) copy-start(s32[4,8]{1,0:T(4,128)} %param.9) | copy-start | bytes 388
Sparse Core Ops, SparseCore 0:
  82.5 28.2 reduce-scatter.1
